TPU v7x, 128 devices: a whole 4x4x4 slice. The times are simulated.
128 devices in a mesh: seq: 32 (over z, y, x_hi), dp: 4 (over x_lo, core).
Axes of the slice: x: 4 (x_hi: 2, x_lo: 2; x = x_hi * 2 + x_lo), y: 4, z: 4, core: 2. Of those that a mesh axis runs over, the one named last changes fastest.
Arguments:
- hidden: bfloat16 [4, 8192, 4608], P('dp', 'seq'), may hold values from -6 to 6
- queries: bfloat16 [4, 8192, 2048], P('dp', 'seq'), may hold values from -64 to 64
- down_weight: bfloat16 [4608, 1024], P('dp'), may hold values from -0.09375 to 0.09375
- up_weight: bfloat16 [2, 512, 1024], P(None, 'dp'), may hold values from -0.25 to 0.25
- lengths: int32 [4], P('dp'), may hold values from 2048 to 8192
Outputs:
- latent_cache: bfloat16 [4, 8192, 1024], P('dp', 'seq')
- attended: bfloat16 [4, 8192, 2048], P('dp', 'seq')
All inputs are finite; a program needn't handle non-finite values.
Results may differ from a plain program's by a relative error of at most 0.012.
The roundings to bfloat16 on the way count: a program that leaves them out, or rounds other values in their place, can miss the bound.
Values may be sent and summed in bfloat16 or wider, within the bound.
No kernel may reach another device: no remote copies, remote signals or barrier semaphores. Data moves between devices by JAX's collectives and lax.ppermute only.
A program may use at most 128 MiB of HBM per device.

v0:
```python
import jax
import jax.numpy as jnp
from jax import lax
from jax.sharding import Mesh
from jax.sharding import PartitionSpec as P

HEAD = 128
WINDOW = 4096
DP = ("dp_0", "dp_1")
query_scale = 144.0 ** (-0.5)
soft_cap = 50.0


def laid_out(pieces, dim):
    lengths = list(pieces.shape[1:])
    lengths[dim] *= pieces.shape[0]
    return jnp.moveaxis(pieces, 0, dim).reshape(lengths)


def stacked_from(array, axes, turns):
    pieces = array
    for k in turns:
        pieces = lax.all_gather(pieces, axes[k])
    done = turns[::-1]
    back = [done.index(k) for k in range(len(axes))]
    pieces = pieces.transpose(*back, *range(len(axes), pieces.ndim))
    return pieces.reshape(-1, *array.shape)


def gathered_by_axis(array, axes, turns, dim):
    return laid_out(stacked_from(array, axes, turns), dim)


def from_everyone(array, axis):
    size = lax.axis_size(axis)
    return lax.all_to_all(
        jnp.broadcast_to(array[None], (size, *array.shape)), axis, 0, 0, tiled=True
    )


def gathered_copies(array, axis, dim):
    return laid_out(from_everyone(array, axis), dim)


def rotate(values_in, start_pos):
    batches, count, width = values_in.shape
    half_head = HEAD // 2
    places = (start_pos + jnp.arange(count, dtype=jnp.int32)).astype(jnp.float32)
    freqs = 10000.0 ** (-2.0 * jnp.arange(half_head, dtype=jnp.float32) / HEAD)
    angles = places[:, None] * freqs[None, :]
    cosine = jnp.cos(angles)[None, :, None, :]
    sine_val = jnp.sin(angles)[None, :, None, :]
    split_heads = values_in.reshape(batches, count, width // HEAD, 2, half_head)
    lower = split_heads[:, :, :, 0, :]
    upper = split_heads[:, :, :, 1, :]
    turned = jnp.stack(
        [lower * cosine - upper * sine_val, upper * cosine + lower * sine_val], axis=3
    )
    return turned.reshape(batches, count, width)


def expand(latent_rows, start_pos, uppers):
    batches, count, latent_rank = latent_rows.shape
    key_rank = latent_rank // 2
    kv_width = uppers.shape[2]
    keys_raw = jnp.dot(
        latent_rows[:, :, :key_rank].reshape(-1, key_rank),
        uppers[0],
        preferred_element_type=jnp.float32,
    )
    keys_out = rotate(keys_raw.reshape(batches, count, kv_width), start_pos).astype(jnp.bfloat16)
    values_out = jnp.dot(
        latent_rows[:, :, key_rank:].reshape(-1, key_rank),
        uppers[1],
        preferred_element_type=jnp.float32,
    )
    values_out = values_out.astype(jnp.bfloat16).reshape(batches, count, kv_width)
    return jnp.stack([keys_out, values_out])


def attend(state, pairs, start_pos, q_split, q_pos):
    numer, denom = state
    batches, count, kv_width = pairs.shape[1:]
    groups = kv_width // HEAD
    keys_grp = pairs[0].reshape(batches, count, groups, HEAD)
    values_grp = pairs[1].reshape(batches, count, groups, HEAD)
    raw = jnp.einsum("blgrd,bngd->bgrln", q_split, keys_grp, preferred_element_type=jnp.float32)
    capped = soft_cap * jnp.tanh(raw * (query_scale / soft_cap))
    key_pos = start_pos + jnp.arange(count, dtype=jnp.int32)
    allowed = (
        (key_pos[None, :] <= q_pos[:, None])
        & (key_pos[None, :] > q_pos[:, None] - WINDOW)
        & (key_pos[None, :] >= 0)
    )
    expo = jnp.where(allowed, jnp.exp(capped), 0.0)
    denom = denom + jnp.sum(expo, axis=-1)
    numer = numer + jnp.einsum(
        "bgrln,bngd->blgrd",
        expo.astype(jnp.bfloat16),
        values_grp,
        preferred_element_type=jnp.float32,
    )
    return (numer, denom)


def body(hidden, queries, down_weight, up_weight, lengths):
    seq_count, local_rows, model_dim = hidden.shape
    latent_rank = down_weight.shape[1]
    flat_hidden = hidden.reshape(seq_count * local_rows, model_dim)
    latent_sum = jnp.dot(
        flat_hidden,
        gathered_by_axis(down_weight, DP, (0, 1), 0),
        preferred_element_type=jnp.float32,
    )
    seq_index = lax.axis_index("seq")
    own_start = seq_index * local_rows
    q_pos = own_start + jnp.arange(local_rows, dtype=jnp.int32)
    is_live = q_pos[None, :] < lengths[:, None]
    latent = latent_sum.astype(jnp.bfloat16).reshape(seq_count, local_rows, latent_rank)
    latent = jnp.where(is_live[:, :, None], latent, jnp.zeros((), jnp.bfloat16))
    uppers = gathered_copies(up_weight, DP, 1)
    groups = up_weight.shape[2] // HEAD
    ratio = queries.shape[2] // (groups * HEAD)
    q_split = queries.reshape(seq_count, local_rows, groups, ratio, HEAD)
    initial = (
        jnp.zeros((seq_count, local_rows, groups, ratio, HEAD), jnp.float32),
        jnp.zeros((seq_count, groups, ratio, local_rows), jnp.float32),
    )

    def unpack(travel, start_pos):
        return expand(travel, start_pos, uppers)

    tile_rows = local_rows * max(1, 512 // local_rows)
    part = lax.all_gather(latent, "seq", axis=1, tiled=True)
    row_axis = part.ndim - 2
    count = part.shape[row_axis]
    pieces = count // tile_rows
    shaped = part.reshape(part.shape[:row_axis] + (pieces, tile_rows) + part.shape[row_axis + 1 :])
    shaped = jnp.moveaxis(shaped, row_axis, 0)

    def scan_step(inner, packed):
        offset, tile_data = packed
        tile_start = offset * tile_rows
        return (attend(inner, unpack(tile_data, tile_start), tile_start, q_split, q_pos), None)

    outcome = lax.scan(scan_step, initial, (jnp.arange(pieces, dtype=jnp.int32), shaped))
    numer, denom = outcome[0]
    result = numer / jnp.transpose(denom, (0, 3, 1, 2))[..., None]
    result = result.reshape(seq_count, local_rows, groups * ratio * HEAD)
    attended = jnp.where(is_live[:, :, None], result, 0.0).astype(jnp.bfloat16)
    return (latent, attended)


def solution(mesh):
    split = Mesh(mesh.devices.reshape(mesh.shape["seq"], 2, 2), ("seq", "dp_0", "dp_1"))
    placed = (P(DP, "seq", None), P(DP, "seq", None), P(DP, None), P(None, DP, None), P(DP))
    return jax.shard_map(
        body,
        mesh=split,
        in_specs=placed,
        out_specs=(P(DP, "seq", None), P(DP, "seq", None)),
        check_vma=False,
    )
```

profile of v0, /device:TPU:0, one launch (start us, length us, event | category | flops | bytes accessed | tf_op | source)
XLA Modules:
  0.0 543.6 jit_solution(10203643698651200933)
XLA Ops:
  8.0 69.3 %all-gather.7.cloned.1.call-done = bf16[2304,1024]{1,0:T(8,128)(2,1)} async-done(((bf16[1152,1024]{1,0:T(8,128)(2,1)}), bf16[2304,1024]{1,0:T(8,128)(2,1)}) %all-gather.7.cloned.1.call-update) | async-done | bytes 4718608 | tf_op jit(solution)/shard_map/all_gather | solution.py:23
  78.0 26.2 %all-gather.9.cloned.1.call-done = bf16[4,1152,1024]{2,1,0:T(8,128)(2,1)} async-done(((bf16[2,1152,1024]{2,1,0:T(8,128)(2,1)}), bf16[4,1152,1024]{2,1,0:T(8,128)(2,1)}) %all-gather.9.cloned.1.call-update) | async-done | bytes 9437200 | tf_op jit(solution)/shard_map/all_gather | solution.py:23
  104.3 8.4 %copy.42 = bf16[2,2,1152,1024]{3,2,1,0:T(8,128)(2,1)} copy(bf16[2,2,1152,1024]{3,2,0,1:T(8,128)(2,1)} %bitcast.131) | data formatting | bytes 18874368 | tf_op jit(solution)/shard_map/transpose | solution.py:26
  112.7 7.1 %fusion.24 = bf16[256,1024]{1,0:T(8,128)(2,1)} fusion(bf16[4608,1024]{1,0:T(8,128)(2,1)} %bitcast.132, bf16[1,256,4608]{2,1,0:T(8,128)(2,1)S(1)} %copy-done, pred[256]{0:T(512)(128)(4,1)S(1)} %add_compare_fusion), kind=kOutput, calls=%fused_computation.37 | convolution fusion | flops 2416443392 | bytes 12321024 | tf_op jit(solution)/shard_map/dot_general | solution.py:110
  120.2 1.6 broadcast_in_dim.69
  121.8 3.6 all-to-all-start
  125.4 1.5 copy.45
  126.9 1.3 copy.48
  128.2 26.6 %all-to-all-done = bf16[4,2,128,1024]{2,3,1,0:T(8,128)(2,1)S(1)} async-done(((bf16[4,2,128,1024]{2,3,1,0:T(8,128)(2,1)}), bf16[4,2,128,1024]{2,3,1,0:T(8,128)(2,1)S(1)}, u32[]{:S(2)}, u32[]{:S(2)}) %all-to-all-start) | async-done | bytes 2097184 | tf_op jit(solution)/shard_map/all_to_all | solution.py:36
  154.8 2.7 copy.44
  157.5 4.0 copy.47
  161.5 120.0 %all-gather.11.cloned.1.call-done = bf16[8192,1024]{1,0:T(8,128)(2,1)} async-done(((bf16[256,1024]{1,0:T(8,128)(2,1)}), bf16[8192,1024]{1,0:T(8,128)(2,1)}) %all-gather.11.cloned.1.call-update) | async-done | bytes 16777232 | tf_op jit(solution)/shard_map/all_gather | solution.py:134
  281.5 249.8 %while.15 = (s32[]{:T(128)}, f32[1,256,8,2,128]{1,4,3,2,0:T(8,128)}, f32[1,8,2,256]{3,2,1,0:T(2,128)S(1)}, bf16[16,1,512,1024]{3,2,1,0:T(8,128)(2,1)}, bf16[2,51...) while((s32[]{:T(128)}, ...), condition=%wide.region_2.3_spmd.clone, body=%wide.region_0.2_spmd.clone.sunk | while | flops 2169018880 | bytes 72300888 | solution.py:146
  283.6 1.3 dynamic-slice_bitcast_fusion.2
  289.5 3.4 fusion.44
  292.9 2.8 bitcast_add_fusion.4
  299.2 1.3 dynamic-slice_bitcast_fusion.2
  305.1 3.4 fusion.44
  308.5 2.8 bitcast_add_fusion.4
  314.8 1.3 dynamic-slice_bitcast_fusion.2
  320.7 3.4 fusion.44
  324.1 2.8 bitcast_add_fusion.4
  330.4 1.3 dynamic-slice_bitcast_fusion.2
  336.3 3.4 fusion.44
  339.8 2.8 bitcast_add_fusion.4
  346.0 1.3 dynamic-slice_bitcast_fusion.2
  351.9 3.4 fusion.44
  355.4 2.8 bitcast_add_fusion.4
  361.6 1.3 dynamic-slice_bitcast_fusion.2
  367.5 3.4 fusion.44
  371.0 2.8 bitcast_add_fusion.4
  377.2 1.3 dynamic-slice_bitcast_fusion.2
  383.1 3.4 fusion.44
  386.6 2.8 bitcast_add_fusion.4
  392.8 1.3 dynamic-slice_bitcast_fusion.2
  398.7 3.4 fusion.44
  402.2 2.8 bitcast_add_fusion.4
  408.5 1.3 dynamic-slice_bitcast_fusion.2
  414.4 3.4 fusion.44
  417.8 2.8 bitcast_add_fusion.4
  424.1 1.3 dynamic-slice_bitcast_fusion.2
  430.0 3.4 fusion.44
  433.4 2.8 bitcast_add_fusion.4
  439.7 1.3 dynamic-slice_bitcast_fusion.2
  445.6 3.4 fusion.44
  449.0 2.8 bitcast_add_fusion.4
  455.3 1.3 dynamic-slice_bitcast_fusion.2
  461.2 3.4 fusion.44
  464.7 2.8 bitcast_add_fusion.4
  470.9 1.3 dynamic-slice_bitcast_fusion.2
  476.8 3.4 fusion.44
  480.3 2.8 bitcast_add_fusion.4
  486.5 1.3 dynamic-slice_bitcast_fusion.2
  492.4 3.4 fusion.44
  495.9 2.8 bitcast_add_fusion.4
  502.1 1.3 dynamic-slice_bitcast_fusion.2
  508.0 3.4 fusion.44
  511.5 2.8 bitcast_add_fusion.4
  517.7 1.3 dynamic-slice_bitcast_fusion.2
  523.6 3.4 fusion.44
  527.1 2.8 bitcast_add_fusion.4
  531.3 1.9 broadcast_divide_fusion
  533.2 1.4 copy.54
  534.7 2.4 select_convert_fusion
  (437 shorter events, 116.5 us)
Async XLA Ops:
  7.2 105.5 %copy-start = (bf16[1,256,4608]{2,1,0:T(8,128)(2,1)S(1)}, bf16[1,256,4608]{2,1,0:T(8,128)(2,1)}, u32[]{:S(2)}) copy-start(bf16[1,256,4608]{2,1,0:T(8,128)(2,1)} %param.7) | copy-start | bytes 7077892
  7.2 70.1 %all-gather.7.cloned.1.call-start = ((), (), s32[]{:S(2)}) async-start(), calls=%async_computation.1 | async-start | bytes 7077888 | tf_op jit(solution)/shard_map/all_gather | solution.py:23
  7.9 96.4 %all-gather.9.cloned.1.call-start = ((), (), s32[]{:S(2)}) async-start(), calls=%async_computation.2 | async-start | bytes 14155776 | tf_op jit(solution)/shard_map/all_gather | solution.py:23
  77.3 204.1 %all-gather.11.cloned.1.call-start = ((), (), s32[]{:S(2)}) async-start(), calls=%async_computation.3 | async-start | bytes 17301504 | tf_op jit(solution)/shard_map/all_gather | solution.py:134
  78.0 34.7 %copy-start.7 = (pred[256]{0:T(512)(128)(4,1)}, pred[256]{0:T(512)(128)(4,1)S(1)}, u32[]{:S(2)}) copy-start(pred[256]{0:T(512)(128)(4,1)S(1)} %add_compare_fusion) | copy-start | bytes 772
  112.7 7.2 %copy-start.6 = (bf16[2,128,1024]{2,1,0:T(8,128)(2,1)S(1)}, bf16[2,128,1024]{2,1,0:T(8,128)(2,1)}, u32[]{:S(2)}) copy-start(bf16[2,128,1024]{2,1,0:T(8,128)(2,1)} %param.10) | copy-start | bytes 1572868
  121.8 33.0 %all-to-all-start = ((bf16[4,2,128,1024]{2,3,1,0:T(8,128)(2,1)}), bf16[4,2,128,1024]{2,3,1,0:T(8,128)(2,1)S(1)}, u32[]{:S(2)}, u32[]{:S(2)}) async-start(bf16[4,2,128,1024]{2,3,1,0:T(8,128)(2,1)} %broadcast_in_dim.69), calls=%async_computation | async-start | bytes 4194304 | tf_op jit(solution)/shard_map/all_to_all | solution.py:36
  281.5 3.4 copy-start.2
  289.5 3.5 copy-start.3
  292.9 4.2 copy-start.10
  297.1 2.1 copy-start.9
  297.1 3.4 copy-start.2
  305.1 3.4 copy-start.3
  308.5 4.2 copy-start.10
  312.7 3.4 copy-start.2
  320.7 3.4 copy-start.3
  324.1 4.2 copy-start.10
  328.3 2.1 copy-start.9
  328.3 3.4 copy-start.2
  336.3 3.4 copy-start.3
  339.8 4.2 copy-start.10
  343.9 2.1 copy-start.9
  343.9 3.4 copy-start.2
  351.9 3.4 copy-start.3
  355.4 4.2 copy-start.10
  359.5 3.4 copy-start.2
  367.5 3.4 copy-start.3
  371.0 4.2 copy-start.10
  375.2 2.1 copy-start.9
  375.2 3.4 copy-start.2
  383.1 3.4 copy-start.3
  386.6 4.2 copy-start.10
  390.8 3.4 copy-start.2
  398.7 3.4 copy-start.3
  402.2 4.2 copy-start.10
  406.4 2.1 copy-start.9
  406.4 3.4 copy-start.2
  414.4 3.4 copy-start.3
  417.8 4.2 copy-start.10
  422.0 3.4 copy-start.2
  430.0 3.4 copy-start.3
  433.4 4.2 copy-start.10
  437.6 2.1 copy-start.9
  437.6 3.4 copy-start.2
  445.6 3.4 copy-start.3
  449.0 4.2 copy-start.10
  453.2 2.1 copy-start.9
  453.2 3.4 copy-start.2
  461.2 3.4 copy-start.3
  464.7 4.2 copy-start.10
  468.8 3.4 copy-start.2
  476.8 3.4 copy-start.3
  480.3 4.2 copy-start.10
  484.4 3.4 copy-start.2
  492.4 3.4 copy-start.3
  495.9 4.2 copy-start.10
  500.1 3.4 copy-start.2
  508.0 3.4 copy-start.3
  511.5 4.2 copy-start.10
  515.7 3.4 copy-start.2
  523.6 3.4 copy-start.3
  527.1 4.2 copy-start.10
  531.3 3.4 copy-start.8
  531.3 5.8 %copy-start.1 = (bf16[1,256,4608]{2,1,0:T(8,128)(2,1)S(1)}, bf16[1,256,4608]{2,1,0:T(8,128)(2,1)}, u32[]{:S(2)}) copy-start(bf16[1,256,4608]{2,1,0:T(8,128)(2,1)} %param.7) | copy-start | bytes 7077892
  (41 other events, 59.2 us)
Sparse Core Ops, SparseCore 0:
  9.6 67.6 all-gather.6
  79.0 25.2 all-gather.8
  120.0 161.4 all-gather.10
where the time goes:
time: 546 us; the launch traced here: 544 us
  waiting for transfers between devices  243 us (45%)
  matrix products  132 us (24%)
  local copies, waits for them, and re-layouts  113 us (21%)
  other arithmetic  24.6 us (5%)
  between operations  14.5 us (3%)
  loops' own time  13.1 us (2%)
    all_gather x1, waiting for transfers between devices, body(): part = lax.all_gather(latent, 'seq', axis=1, tiled=True)  120 us
    all_gather x2, waiting for transfers between devices, stacked_from(): pieces = lax.all_gather(pieces, axes[k])  95.6 us
    dot_general x16, matrix products, attend(): jnp.einsum('blgrd,bngd->bgrln', q_split, keys_grp, preferred_element_type...  55 us
    dot_general x16, matrix products, attend(): jnp.einsum('bgrln,bngd->blgrd', expo.astype(jnp.bfloat16), values_grp, pr...  45.5 us
    while x192, local copies, waits for them, and re-layouts  32.4 us
    all_to_all x1, waiting for transfers between devices, from_everyone(): lax.all_to_all(jnp.broadcast_to(array[None], (size, *array.shape)), axis,...  26.6 us
    squeeze x16, local copies, waits for them, and re-layouts, body(): lax.scan(scan_step, initial, (jnp.arange(pieces, dtype=jnp.int32), shaped))  20.8 us
    slice x16, local copies, waits for them, and re-layouts, expand(): uppers[0]  20.7 us
  transfers between devices with their start and end apart: 4, of which 4 were waited for; matrix products, arithmetic and copies ran while one was open for 2% of the time, Pallas kernels for 0%

commit v1 on v0

--- a/solution.py
+++ b/solution.py
@@ -131,7 +131,8 @@
         return expand(travel, start_pos, uppers)
 
     tile_rows = local_rows * max(1, 512 // local_rows)
-    part = lax.all_gather(latent, "seq", axis=1, tiled=True)
+    stack = jnp.stack([latent] * lax.axis_size("seq"))
+    part = jnp.concatenate(lax.all_to_all(stack, "seq", 0, 0), axis=1)
     row_axis = part.ndim - 2
     count = part.shape[row_axis]
     pieces = count // tile_rows

time: 546 us -> 758 us (1.39)
  the two profiles are of different devices: /device:TPU:0 before, /device:TPU:60 now
where the time goes in v1:
time: 758 us; the launch traced here: 756 us
  waiting for transfers between devices  372 us (49%)
  matrix products  235 us (31%)
  local copies, waits for them, and re-layouts  84.4 us (11%)
  other arithmetic  24.5 us (3%)
  between operations  14.8 us (2%)
  starting transfers between devices  14.5 us (2%)
  loops' own time  10.9 us (1%)
    all_to_all x1, waiting for transfers between devices, body(): part = jnp.concatenate(lax.all_to_all(stack, 'seq', 0, 0), axis=1)  282 us
    dot_general x16, matrix products, attend(): jnp.einsum('bgrln,bngd->blgrd', expo.astype(jnp.bfloat16), values_grp, pr...  127 us
    all_gather x2, waiting for transfers between devices, stacked_from(): pieces = lax.all_gather(pieces, axes[k])  88.6 us
    dot_general x16, matrix products, attend(): jnp.einsum('blgrd,bngd->bgrln', q_split, keys_grp, preferred_element_type...  78.3 us
    squeeze x16, local copies, waits for them, and re-layouts, body(): lax.scan(scan_step, initial, (jnp.arange(pieces, dtype=jnp.int32), shaped))  20.8 us
    slice x16, local copies, waits for them, and re-layouts, expand(): uppers[0]  20.7 us
  transfers between devices with their start and end apart: 4, of which 3 were waited for; matrix products, arithmetic and copies ran while one was open for 3% of the time, Pallas kernels for 0%

profile of v1, /device:TPU:60, one launch (start us, length us, event | category | flops | bytes accessed | tf_op | source)
XLA Modules:
  0.0 755.7 jit_solution(16736941010433916315)
XLA Ops:
  8.0 68.3 %all-gather.5.cloned.1.call-done = bf16[2304,1024]{1,0:T(8,128)(2,1)} async-done(((bf16[1152,1024]{1,0:T(8,128)(2,1)}), bf16[2304,1024]{1,0:T(8,128)(2,1)}) %all-gather.5.cloned.1.call-update) | async-done | bytes 4718608 | tf_op jit(solution)/shard_map/all_gather | solution.py:23
  76.5 1.6 broadcast_in_dim.69
  78.1 4.4 all-to-all-start.1
  83.2 20.4 %all-gather.7.cloned.1.call-done = bf16[4,1152,1024]{2,1,0:T(8,128)(2,1)} async-done(((bf16[2,1152,1024]{2,1,0:T(8,128)(2,1)}), bf16[4,1152,1024]{2,1,0:T(8,128)(2,1)}) %all-gather.7.cloned.1.call-update) | async-done | bytes 9437200 | tf_op jit(solution)/shard_map/all_gather | solution.py:23
  103.6 8.5 %copy.39 = bf16[2,2,1152,1024]{3,2,1,0:T(8,128)(2,1)} copy(bf16[2,2,1152,1024]{3,2,0,1:T(8,128)(2,1)} %bitcast.131) | data formatting | bytes 18874368 | tf_op jit(solution)/shard_map/transpose | solution.py:26
  112.1 6.3 fusion.24
  118.4 6.1 stack.8
  124.5 10.0 %all-to-all-start = ((bf16[32,1,256,1024]{3,2,1,0:T(8,128)(2,1)}), bf16[32,1,256,1024]{3,2,1,0:T(8,128)(2,1)}, u32[]{:S(2)}, u32[]{:S(2)}) async-start(bf16[32,1,256,1024]{3,2,1,0:T(8,128)(2,1)} %stack.8), calls=%async_computation | async-start | bytes 33554432 | tf_op jit(solution)/shard_map/all_to_all | solution.py:135
  135.8 3.0 copy.41
  138.8 2.6 copy.44
  141.4 282.3 %all-to-all-done = bf16[32,1,256,1024]{3,2,1,0:T(8,128)(2,1)} async-done(((bf16[32,1,256,1024]{3,2,1,0:T(8,128)(2,1)}), bf16[32,1,256,1024]{3,2,1,0:T(8,128)(2,1)}, u32[]{:S(2)}, u32[]{:S(2)}) %all-to-all-start) | async-done | bytes 16777248 | tf_op jit(solution)/shard_map/all_to_all | solution.py:135
  423.7 319.4 %while.15 = (s32[]{:T(128)}, f32[1,256,8,2,128]{1,4,3,2,0:T(8,128)}, f32[1,8,2,256]{3,2,1,0:T(2,128)S(1)}, bf16[16,1,512,1024]{3,2,1,0:T(8,128)(2,1)}, bf16[2,51...) while((s32[]{:T(128)}, ...), condition=%wide.region_2.3_spmd.clone, body=%wide.region_0.2_spmd.clone.sunk | while | flops 2169018880 | bytes 51328696 | solution.py:147
  425.4 1.3 dynamic-slice_bitcast_fusion.2
  426.7 1.3 slice.69
  429.5 4.9 fusion.44
  435.7 7.4 bitcast_add_fusion.4
  444.8 1.3 dynamic-slice_bitcast_fusion.2
  448.9 4.9 fusion.44
  455.1 8.0 %bitcast_add_fusion.4 = f32[1,256,8,2,128]{1,4,3,2,0:T(8,128)} fusion(f32[1,256,8,2,128]{1,4,3,2,0:T(8,128)} %get-tuple-element.276, bf16[512,8,128,1]{0,2,3,1:T(8,128)(2,1)S(1)} %bitcast.130, f32[8,512,256,2]{2,1,3,0:T(8,128)} %get-tuple-element.262, pred[256,512]{0,1:T(8,128)(4,1)S(1)} %and_and_fusion.2, pred[]{:T(512)S(6)} %compare.3), kind=kOutput, calls=%fused_computation.7.clone.1 | convolution fusion | flops 546308096 | bytes 13762561 | tf_op jit(solution)/shard_map/while/body/eval_jaxpr/bgrln,bngd->blgrd/dot_general | solution.py:97
  464.8 1.3 dynamic-slice_bitcast_fusion.2
  468.9 4.9 fusion.44
  475.1 8.0 %bitcast_add_fusion.4 = f32[1,256,8,2,128]{1,4,3,2,0:T(8,128)} fusion(f32[1,256,8,2,128]{1,4,3,2,0:T(8,128)} %get-tuple-element.276, bf16[512,8,128,1]{0,2,3,1:T(8,128)(2,1)S(1)} %bitcast.130, f32[8,512,256,2]{2,1,3,0:T(8,128)} %get-tuple-element.262, pred[256,512]{0,1:T(8,128)(4,1)S(1)} %and_and_fusion.2, pred[]{:T(512)S(6)} %compare.3), kind=kOutput, calls=%fused_computation.7.clone.1 | convolution fusion | flops 546308096 | bytes 13762561 | tf_op jit(solution)/shard_map/while/body/eval_jaxpr/bgrln,bngd->blgrd/dot_general | solution.py:97
  484.8 1.3 dynamic-slice_bitcast_fusion.2
  488.9 4.9 fusion.44
  495.1 8.0 %bitcast_add_fusion.4 = f32[1,256,8,2,128]{1,4,3,2,0:T(8,128)} fusion(f32[1,256,8,2,128]{1,4,3,2,0:T(8,128)} %get-tuple-element.276, bf16[512,8,128,1]{0,2,3,1:T(8,128)(2,1)S(1)} %bitcast.130, f32[8,512,256,2]{2,1,3,0:T(8,128)} %get-tuple-element.262, pred[256,512]{0,1:T(8,128)(4,1)S(1)} %and_and_fusion.2, pred[]{:T(512)S(6)} %compare.3), kind=kOutput, calls=%fused_computation.7.clone.1 | convolution fusion | flops 546308096 | bytes 13762561 | tf_op jit(solution)/shard_map/while/body/eval_jaxpr/bgrln,bngd->blgrd/dot_general | solution.py:97
  504.8 1.3 dynamic-slice_bitcast_fusion.2
  508.9 4.9 fusion.44
  515.1 8.0 %bitcast_add_fusion.4 = f32[1,256,8,2,128]{1,4,3,2,0:T(8,128)} fusion(f32[1,256,8,2,128]{1,4,3,2,0:T(8,128)} %get-tuple-element.276, bf16[512,8,128,1]{0,2,3,1:T(8,128)(2,1)S(1)} %bitcast.130, f32[8,512,256,2]{2,1,3,0:T(8,128)} %get-tuple-element.262, pred[256,512]{0,1:T(8,128)(4,1)S(1)} %and_and_fusion.2, pred[]{:T(512)S(6)} %compare.3), kind=kOutput, calls=%fused_computation.7.clone.1 | convolution fusion | flops 546308096 | bytes 13762561 | tf_op jit(solution)/shard_map/while/body/eval_jaxpr/bgrln,bngd->blgrd/dot_general | solution.py:97
  524.8 1.3 dynamic-slice_bitcast_fusion.2
  528.9 4.9 fusion.44
  535.1 8.0 %bitcast_add_fusion.4 = f32[1,256,8,2,128]{1,4,3,2,0:T(8,128)} fusion(f32[1,256,8,2,128]{1,4,3,2,0:T(8,128)} %get-tuple-element.276, bf16[512,8,128,1]{0,2,3,1:T(8,128)(2,1)S(1)} %bitcast.130, f32[8,512,256,2]{2,1,3,0:T(8,128)} %get-tuple-element.262, pred[256,512]{0,1:T(8,128)(4,1)S(1)} %and_and_fusion.2, pred[]{:T(512)S(6)} %compare.3), kind=kOutput, calls=%fused_computation.7.clone.1 | convolution fusion | flops 546308096 | bytes 13762561 | tf_op jit(solution)/shard_map/while/body/eval_jaxpr/bgrln,bngd->blgrd/dot_general | solution.py:97
  544.8 1.3 dynamic-slice_bitcast_fusion.2
  548.9 4.9 fusion.44
  555.1 8.0 %bitcast_add_fusion.4 = f32[1,256,8,2,128]{1,4,3,2,0:T(8,128)} fusion(f32[1,256,8,2,128]{1,4,3,2,0:T(8,128)} %get-tuple-element.276, bf16[512,8,128,1]{0,2,3,1:T(8,128)(2,1)S(1)} %bitcast.130, f32[8,512,256,2]{2,1,3,0:T(8,128)} %get-tuple-element.262, pred[256,512]{0,1:T(8,128)(4,1)S(1)} %and_and_fusion.2, pred[]{:T(512)S(6)} %compare.3), kind=kOutput, calls=%fused_computation.7.clone.1 | convolution fusion | flops 546308096 | bytes 13762561 | tf_op jit(solution)/shard_map/while/body/eval_jaxpr/bgrln,bngd->blgrd/dot_general | solution.py:97
  564.8 1.3 dynamic-slice_bitcast_fusion.2
  568.9 4.9 fusion.44
  575.1 8.0 %bitcast_add_fusion.4 = f32[1,256,8,2,128]{1,4,3,2,0:T(8,128)} fusion(f32[1,256,8,2,128]{1,4,3,2,0:T(8,128)} %get-tuple-element.276, bf16[512,8,128,1]{0,2,3,1:T(8,128)(2,1)S(1)} %bitcast.130, f32[8,512,256,2]{2,1,3,0:T(8,128)} %get-tuple-element.262, pred[256,512]{0,1:T(8,128)(4,1)S(1)} %and_and_fusion.2, pred[]{:T(512)S(6)} %compare.3), kind=kOutput, calls=%fused_computation.7.clone.1 | convolution fusion | flops 546308096 | bytes 13762561 | tf_op jit(solution)/shard_map/while/body/eval_jaxpr/bgrln,bngd->blgrd/dot_general | solution.py:97
  584.8 1.3 dynamic-slice_bitcast_fusion.2
  588.9 4.9 fusion.44
  595.1 8.0 %bitcast_add_fusion.4 = f32[1,256,8,2,128]{1,4,3,2,0:T(8,128)} fusion(f32[1,256,8,2,128]{1,4,3,2,0:T(8,128)} %get-tuple-element.276, bf16[512,8,128,1]{0,2,3,1:T(8,128)(2,1)S(1)} %bitcast.130, f32[8,512,256,2]{2,1,3,0:T(8,128)} %get-tuple-element.262, pred[256,512]{0,1:T(8,128)(4,1)S(1)} %and_and_fusion.2, pred[]{:T(512)S(6)} %compare.3), kind=kOutput, calls=%fused_computation.7.clone.1 | convolution fusion | flops 546308096 | bytes 13762561 | tf_op jit(solution)/shard_map/while/body/eval_jaxpr/bgrln,bngd->blgrd/dot_general | solution.py:97
  604.8 1.3 dynamic-slice_bitcast_fusion.2
  608.9 4.9 fusion.44
  615.1 8.0 %bitcast_add_fusion.4 = f32[1,256,8,2,128]{1,4,3,2,0:T(8,128)} fusion(f32[1,256,8,2,128]{1,4,3,2,0:T(8,128)} %get-tuple-element.276, bf16[512,8,128,1]{0,2,3,1:T(8,128)(2,1)S(1)} %bitcast.130, f32[8,512,256,2]{2,1,3,0:T(8,128)} %get-tuple-element.262, pred[256,512]{0,1:T(8,128)(4,1)S(1)} %and_and_fusion.2, pred[]{:T(512)S(6)} %compare.3), kind=kOutput, calls=%fused_computation.7.clone.1 | convolution fusion | flops 546308096 | bytes 13762561 | tf_op jit(solution)/shard_map/while/body/eval_jaxpr/bgrln,bngd->blgrd/dot_general | solution.py:97
  624.8 1.3 dynamic-slice_bitcast_fusion.2
  628.9 4.9 fusion.44
  635.1 8.0 %bitcast_add_fusion.4 = f32[1,256,8,2,128]{1,4,3,2,0:T(8,128)} fusion(f32[1,256,8,2,128]{1,4,3,2,0:T(8,128)} %get-tuple-element.276, bf16[512,8,128,1]{0,2,3,1:T(8,128)(2,1)S(1)} %bitcast.130, f32[8,512,256,2]{2,1,3,0:T(8,128)} %get-tuple-element.262, pred[256,512]{0,1:T(8,128)(4,1)S(1)} %and_and_fusion.2, pred[]{:T(512)S(6)} %compare.3), kind=kOutput, calls=%fused_computation.7.clone.1 | convolution fusion | flops 546308096 | bytes 13762561 | tf_op jit(solution)/shard_map/while/body/eval_jaxpr/bgrln,bngd->blgrd/dot_general | solution.py:97
  644.8 1.3 dynamic-slice_bitcast_fusion.2
  648.9 4.9 fusion.44
  655.1 8.0 %bitcast_add_fusion.4 = f32[1,256,8,2,128]{1,4,3,2,0:T(8,128)} fusion(f32[1,256,8,2,128]{1,4,3,2,0:T(8,128)} %get-tuple-element.276, bf16[512,8,128,1]{0,2,3,1:T(8,128)(2,1)S(1)} %bitcast.130, f32[8,512,256,2]{2,1,3,0:T(8,128)} %get-tuple-element.262, pred[256,512]{0,1:T(8,128)(4,1)S(1)} %and_and_fusion.2, pred[]{:T(512)S(6)} %compare.3), kind=kOutput, calls=%fused_computation.7.clone.1 | convolution fusion | flops 546308096 | bytes 13762561 | tf_op jit(solution)/shard_map/while/body/eval_jaxpr/bgrln,bngd->blgrd/dot_general | solution.py:97
  664.8 1.3 dynamic-slice_bitcast_fusion.2
  668.9 4.9 fusion.44
  675.1 8.0 %bitcast_add_fusion.4 = f32[1,256,8,2,128]{1,4,3,2,0:T(8,128)} fusion(f32[1,256,8,2,128]{1,4,3,2,0:T(8,128)} %get-tuple-element.276, bf16[512,8,128,1]{0,2,3,1:T(8,128)(2,1)S(1)} %bitcast.130, f32[8,512,256,2]{2,1,3,0:T(8,128)} %get-tuple-element.262, pred[256,512]{0,1:T(8,128)(4,1)S(1)} %and_and_fusion.2, pred[]{:T(512)S(6)} %compare.3), kind=kOutput, calls=%fused_computation.7.clone.1 | convolution fusion | flops 546308096 | bytes 13762561 | tf_op jit(solution)/shard_map/while/body/eval_jaxpr/bgrln,bngd->blgrd/dot_general | solution.py:97
  684.8 1.3 dynamic-slice_bitcast_fusion.2
  688.9 4.9 fusion.44
  695.1 8.0 %bitcast_add_fusion.4 = f32[1,256,8,2,128]{1,4,3,2,0:T(8,128)} fusion(f32[1,256,8,2,128]{1,4,3,2,0:T(8,128)} %get-tuple-element.276, bf16[512,8,128,1]{0,2,3,1:T(8,128)(2,1)S(1)} %bitcast.130, f32[8,512,256,2]{2,1,3,0:T(8,128)} %get-tuple-element.262, pred[256,512]{0,1:T(8,128)(4,1)S(1)} %and_and_fusion.2, pred[]{:T(512)S(6)} %compare.3), kind=kOutput, calls=%fused_computation.7.clone.1 | convolution fusion | flops 546308096 | bytes 13762561 | tf_op jit(solution)/shard_map/while/body/eval_jaxpr/bgrln,bngd->blgrd/dot_general | solution.py:97
  704.8 1.3 dynamic-slice_bitcast_fusion.2
  708.9 4.9 fusion.44
  715.1 8.0 %bitcast_add_fusion.4 = f32[1,256,8,2,128]{1,4,3,2,0:T(8,128)} fusion(f32[1,256,8,2,128]{1,4,3,2,0:T(8,128)} %get-tuple-element.276, bf16[512,8,128,1]{0,2,3,1:T(8,128)(2,1)S(1)} %bitcast.130, f32[8,512,256,2]{2,1,3,0:T(8,128)} %get-tuple-element.262, pred[256,512]{0,1:T(8,128)(4,1)S(1)} %and_and_fusion.2, pred[]{:T(512)S(6)} %compare.3), kind=kOutput, calls=%fused_computation.7.clone.1 | convolution fusion | flops 546308096 | bytes 13762561 | tf_op jit(solution)/shard_map/while/body/eval_jaxpr/bgrln,bngd->blgrd/dot_general | solution.py:97
  724.8 1.3 dynamic-slice_bitcast_fusion.2
  728.9 4.9 fusion.44
  735.1 8.0 %bitcast_add_fusion.4 = f32[1,256,8,2,128]{1,4,3,2,0:T(8,128)} fusion(f32[1,256,8,2,128]{1,4,3,2,0:T(8,128)} %get-tuple-element.276, bf16[512,8,128,1]{0,2,3,1:T(8,128)(2,1)S(1)} %bitcast.130, f32[8,512,256,2]{2,1,3,0:T(8,128)} %get-tuple-element.262, pred[256,512]{0,1:T(8,128)(4,1)S(1)} %and_and_fusion.2, pred[]{:T(512)S(6)} %compare.3), kind=kOutput, calls=%fused_computation.7.clone.1 | convolution fusion | flops 546308096 | bytes 13762561 | tf_op jit(solution)/shard_map/while/body/eval_jaxpr/bgrln,bngd->blgrd/dot_general | solution.py:97
  743.1 1.9 broadcast_divide_fusion
  745.0 1.4 copy.51
  746.5 2.4 select_convert_fusion
  (277 shorter events, 83.8 us)
Async XLA Ops:
  7.2 104.9 %copy-start = (bf16[1,256,4608]{2,1,0:T(8,128)(2,1)S(1)}, bf16[1,256,4608]{2,1,0:T(8,128)(2,1)}, u32[]{:S(2)}) copy-start(bf16[1,256,4608]{2,1,0:T(8,128)(2,1)} %param.7) | copy-start | bytes 7077892
  7.2 69.1 %copy-start.5 = (bf16[2,128,1024]{2,1,0:T(8,128)(2,1)S(1)}, bf16[2,128,1024]{2,1,0:T(8,128)(2,1)}, u32[]{:S(2)}) copy-start(bf16[2,128,1024]{2,1,0:T(8,128)(2,1)} %param.10) | copy-start | bytes 1572868
  7.2 69.0 %all-gather.5.cloned.1.call-start = ((), (), s32[]{:S(2)}) async-start(), calls=%async_computation.2 | async-start | bytes 7077888 | tf_op jit(solution)/shard_map/all_gather | solution.py:23
  7.9 95.7 %all-gather.7.cloned.1.call-start = ((), (), s32[]{:S(2)}) async-start(), calls=%async_computation.3 | async-start | bytes 14155776 | tf_op jit(solution)/shard_map/all_gather | solution.py:23
  78.1 40.2 %all-to-all-start.1 = ((bf16[4,2,128,1024]{2,3,1,0:T(8,128)(2,1)}), bf16[4,2,128,1024]{2,3,1,0:T(8,128)(2,1)}, u32[]{:S(2)}, u32[]{:S(2)}) async-start(bf16[4,2,128,1024]{2,3,1,0:T(8,128)(2,1)} %broadcast_in_dim.69), calls=%async_computation.1 | async-start | bytes 4194304 | tf_op jit(solution)/shard_map/all_to_all | solution.py:36
  118.3 6.2 copy-start.4
  124.5 10.1 %copy-start.3 = (bf16[1,256,2048]{2,1,0:T(8,128)(2,1)S(1)}, bf16[1,256,2048]{2,1,0:T(8,128)(2,1)}, u32[]{:S(2)}) copy-start(bf16[1,256,2048]{2,1,0:T(8,128)(2,1)} %param.8) | copy-start | bytes 3145732
  124.5 299.2 %all-to-all-start = ((bf16[32,1,256,1024]{3,2,1,0:T(8,128)(2,1)}), bf16[32,1,256,1024]{3,2,1,0:T(8,128)(2,1)}, u32[]{:S(2)}, u32[]{:S(2)}) async-start(bf16[32,1,256,1024]{3,2,1,0:T(8,128)(2,1)} %stack.8), calls=%async_computation | async-start | bytes 33554432 | tf_op jit(solution)/shard_map/all_to_all | solution.py:135
  429.5 4.9 copy-start.2
  448.9 4.9 copy-start.2
  468.9 4.9 copy-start.2
  488.9 4.9 copy-start.2
  508.9 4.9 copy-start.2
  528.9 4.9 copy-start.2
  548.9 4.9 copy-start.2
  568.9 4.9 copy-start.2
  588.9 4.9 copy-start.2
  608.9 4.9 copy-start.2
  628.9 4.9 copy-start.2
  648.9 4.9 copy-start.2
  668.9 4.9 copy-start.2
  688.9 4.9 copy-start.2
  708.9 4.9 copy-start.2
  728.9 4.9 copy-start.2
  743.1 5.8 copy-start.1
Sparse Core Ops, SparseCore 0:
  9.6 66.5 all-gather.4
  77.9 25.6 all-gather.6
